TPU v7x, 32 devices: a whole 2x2x4 slice. The times are simulated.
32 devices in a mesh: grp: 2 (over x), wide: 16 (over z, y, core).
Axes of the slice: x: 2, y: 2, z: 4, core: 2. Of those that a mesh axis runs over, the one named last changes fastest.
Arguments:
- x_pool: bfloat16 [16384, 7168], P(('grp', 'wide')), may hold values from -6 to 6
- token_ids: int32 [4096], P(('grp', 'wide')), may hold values from 0 to 16383, as said below
- cotangent: bfloat16 [4096, 7168], P(('grp', 'wide')), may hold values from -6 to 6
- gate_up: bfloat16 [2, 1024, 7168], P(None, 'wide', 'grp'), may hold values from -0.0625 to 0.0625
- down_weight: bfloat16 [1024, 7168], P('wide', 'grp'), may hold values from -0.1875 to 0.1875
- loss_exponent: int32 [1], replicated, may hold values from 3 to 9
Outputs:
- grad_gate_up: bfloat16 [2, 1024, 7168], P(None, 'wide', 'grp')
- grad_down: bfloat16 [1024, 7168], P('wide', 'grp')
Inputs may be any that keep to these rules, and one draw needn't show every extreme that they name: The 128 ids in aligned block b of token_ids name rows b * 512 to (b + 1) * 512 - 1 of x_pool.
All inputs are finite; a program needn't handle non-finite values.
Results may differ from a plain program's by a relative error of at most 0.014.
Values may be sent and summed in bfloat16 or wider, within the bound.
A program may use at most 192 MiB of HBM per device.

v0:
```python
import functools

import jax
import jax.numpy as jnp
from jax import lax
from jax.experimental import pallas as pl
from jax.experimental.pallas import tpu as pltpu
from jax.sharding import PartitionSpec as P

MESH = pl.DeviceIdType.MESH
NT = (((1,), (1,)), ((), ()))
NN = (((1,), (0,)), ((), ()))
CHUNKS = 2


def line_of(wide_count):
    bits = wide_count.bit_length() - 1
    near_bits = bits - bits // 2
    return wide_count // 2**near_bits, near_bits


def low_bit(mask, bits):
    return (mask & -mask).bit_length() - 1 if mask else bits


def dot(left_side, right_side, dims):
    return lax.dot_general(left_side, right_side, dims, preferred_element_type=jnp.float32)


def token_plan(near_bits):
    near = 2**near_bits
    sends = [("x", 0, 0)]
    for rel in range(2):
        for mask in range(near):
            sends += [(rel, mask, bit) for bit in range(low_bit(mask, near_bits))]
    masks = [mask for mask in range(2, near, 2)]
    masks.sort(key=lambda mask: (bin(mask).count("1"), -mask))
    keyed = [(0, mask) for mask in masks] + [(1, mask) for mask in [0] + masks]
    keyed.sort(key=lambda item: bin(item[1]).count("1") * 2 + (item[0] * 2 if item[1] else 0))
    relays = [(1 + 2 * CHUNKS * (index // 2), rel, mask) for index, (rel, mask) in enumerate(keyed)]
    return sends, relays


def kernel(
    near_bits,
    rows,
    ids_ref,
    expo_ref,
    pool_ref,
    cot_ref,
    gate_up_ref,
    down_ref,
    out_ref,
    tok_x,
    tok_c,
    far_x,
    pool_buf,
    weights,
    grads,
    from_left,
    from_right,
    own_part,
    sent_part,
    got_part,
    deltas,
    acc,
    out_buf,
    send_w,
    recv_w,
    send_t,
    recv_t,
    send_p,
    recv_p,
    send_g,
    recv_g,
    local_sem,
    pool_sem,
    out_sem,
):
    near = 2**near_bits
    wide_count = rows * near
    grp = lax.axis_index("grp")
    wide = lax.axis_index("wide")
    other = 1 - grp
    row = wide // near
    slot = wide % near
    last = rows - 1
    per_dev, _ = ids_ref.shape
    pool_rows = pool_ref.shape[0]
    half = tok_x.shape[1]
    units = gate_up_ref.shape[1]
    span = rows * units
    group_rows = max(1, min(rows, 128 // units))
    groups = rows // group_rows
    lanes = group_rows * units
    cut = per_dev // CHUNKS
    block = 2 * per_dev
    tile = 512

    bit_of = [(slot // 2**bit) % 2 for bit in range(near_bits)]

    def flipped(mask):
        place = slot
        for bit in range(near_bits):
            if mask >> bit & 1:
                place = place + 2**bit * (1 - 2 * bit_of[bit])
        return place

    across = {"grp": other}
    left = {"wide": jnp.maximum(wide - near, 0)}
    right = {"wide": jnp.minimum(wide + near, wide_count - 1)}
    partner = [{"wide": row * near + flipped(2**bit)} for bit in range(near_bits)]

    barrier = pltpu.get_barrier_semaphore()

    def greet(device):
        pl.semaphore_signal(barrier, inc=1, device_id=device, device_id_type=MESH)

    for device in [across] + partner:
        greet(device)

    @pl.when(row > 0)
    def _():
        greet(left)

    @pl.when(row < last)
    def _():
        greet(right)

    neighbours = (row + last) // rows + (2 * last - row) // rows
    pl.semaphore_wait(barrier, 1 + near_bits + neighbours)

    def remote(source, target, sent, received, device):
        return pltpu.make_async_remote_copy(
            src_ref=source,
            dst_ref=target,
            send_sem=sent,
            recv_sem=received,
            device_id=device,
            device_id_type=MESH,
        )

    def unit_rows(origin):
        return pl.ds(pl.multiple_of(origin * units, units), units)

    def weight_copy(direction, hop, kind, source=None):
        going_right = direction == 0
        origin = row - hop if going_right else row + hop
        origin = jnp.clip(origin, 0, last)
        place = weights.at[kind, unit_rows(origin)]
        return remote(
            place if source is None else source,
            place,
            send_w.at[direction, hop, kind],
            recv_w.at[direction, hop, kind],
            right if going_right else left,
        )

    def weight_sends(direction, hop):
        going_right = direction == 0
        held = row >= hop if going_right else row <= last - hop
        open_end = row < last if going_right else row > 0
        return jnp.logical_and(held, open_end)

    def weight_arrives(direction, hop):
        return row >= hop + 1 if direction == 0 else row <= last - hop - 1

    def weight_arrival(direction, hop, kind):
        origin = row - hop - 1 if direction == 0 else row + hop + 1
        place = weights.at[kind, unit_rows(jnp.clip(origin, 0, last))]
        device = left if direction == 0 else right
        return remote(
            place, place, send_w.at[direction, hop, kind], recv_w.at[direction, hop, kind], device
        )

    def weight_source(kind):
        return gate_up_ref.at[kind] if kind < 2 else down_ref

    for kind in range(3):
        for direction in range(2):

            @pl.when(weight_sends(direction, 0))
            def _(kind=kind, direction=direction):
                weight_copy(direction, 0, kind, weight_source(kind)).start()

    sends, relays = token_plan(near_bits)
    send_index = {key: index for index, key in enumerate(sends)}
    buffers = (tok_c, tok_x)

    def token_rows(rel, mask, chunk):
        base = (grp if rel == 0 else other) * near + flipped(mask)
        return pl.ds(pl.multiple_of(base * per_dev + chunk * cut, cut), cut)

    def token_copy(array, chunk, key, source=None):
        rel, mask, bit = key
        if rel == "x":
            place = buffers[array].at[token_rows(0, 0, chunk)]
            device, arrives = across, near
        else:
            place = buffers[array].at[token_rows(rel, mask, chunk)]
            device, arrives = partner[bit], rel * near + mask + 2**bit
        return remote(
            place if source is None else source,
            place,
            send_t.at[array, chunk, send_index[key]],
            recv_t.at[array, chunk, arrives],
            device,
        )

    def token_arrival(array, chunk, rel, mask):
        place = buffers[array].at[token_rows(rel, mask, chunk)]
        device = across if mask == 0 else partner[low_bit(mask, near_bits)]
        return remote(
            place,
            place,
            send_t.at[array, chunk, 0],
            recv_t.at[array, chunk, rel * near + mask],
            device,
        )

    def half_of(which):
        return pl.ds(pl.multiple_of(which * half, half), half)

    pool_far = pltpu.make_async_copy(pool_ref.at[:, half_of(other)], pool_buf, pool_sem.at[0])
    pool_far.start()
    for chunk in range(CHUNKS):
        piece = pl.ds(chunk * cut, cut)
        token_copy(0, chunk, ("x", 0, 0), cot_ref.at[piece, half_of(other)]).start()
        for bit in reversed(range(near_bits)):
            token_copy(0, chunk, (0, 0, bit), cot_ref.at[piece, half_of(grp)]).start()
    local = [
        pltpu.make_async_copy(
            weight_source(kind), weights.at[kind, unit_rows(row)], local_sem.at[kind]
        )
        for kind in range(3)
    ]
    own_rows = pl.ds(pl.multiple_of((grp * near + slot) * per_dev, per_dev), per_dev)
    local.append(
        pltpu.make_async_copy(cot_ref.at[:, half_of(grp)], tok_c.at[own_rows], local_sem.at[3])
    )
    for copy in local:
        copy.start()

    first_row = (grp * wide_count + wide) * pool_rows
    named = ids_ref[...] - first_row
    pick = (named == lax.broadcasted_iota(jnp.int32, (per_dev, pool_rows), 1)).astype(jnp.bfloat16)

    def pick_into(target, offset):
        @pl.loop(0, half // tile)
        def _(index):
            columns = pl.ds(pl.multiple_of(index * tile, tile), tile)
            target[pl.ds(offset, per_dev), columns] = dot(pick, pool_buf[:, columns], NN).astype(
                jnp.bfloat16
            )

    pool_far.wait()
    pick_into(far_x, 0)
    pool_own = pltpu.make_async_copy(pool_ref.at[:, half_of(grp)], pool_buf, pool_sem.at[1])
    pool_own.start()
    for chunk in range(CHUNKS):
        token_copy(1, chunk, ("x", 0, 0), far_x.at[pl.ds(chunk * cut, cut)]).start()
    pool_own.wait()
    pick_into(tok_x, pl.multiple_of((grp * near + slot) * per_dev, per_dev))
    for chunk in range(CHUNKS):
        for bit in reversed(range(near_bits)):
            token_copy(1, chunk, (0, 0, bit)).start()
    for copy in local:
        copy.wait()

    exponent = expo_ref[0]
    unscale = jnp.float32(1.0)
    for bit in range(4):
        factor = jnp.where((exponent // 2**bit) % 2 == 1, jnp.float32(0.5 ** (2**bit)), jnp.float32(1.0))
        unscale = unscale * factor

    own_group = row // group_rows

    def group_at(order):
        return (own_group + order) % groups

    def group_span(order):
        return pl.ds(pl.multiple_of(group_at(order) * lanes, lanes), lanes)

    blocks = [(rel, mask) for rel in range(2) for mask in range(0, near, 2)]

    def part_copy(order, rel, mask, outgoing=True):
        where = block_rows(rel, mask)
        received = (1 - rel if outgoing else rel, mask)
        return remote(
            sent_part.at[order, where],
            got_part.at[order, where],
            send_p.at[order, blocks.index((rel, mask))],
            recv_p.at[order, blocks.index(received)],
            across,
        )

    def block_rows(rel, mask):
        base = (grp if rel == 0 else other) * near + flipped(mask) - bit_of[0]
        return pl.ds(pl.multiple_of(base * per_dev, block), block)

    def forward(order, rel, mask):
        where = block_rows(rel, mask)
        hidden = group_span(order)
        pair = weights[0:2, hidden, :].reshape(2 * lanes, half)
        acts = dot(tok_x[where, :], pair, NT)
        down = dot(tok_c[where, :], weights[2, hidden, :], NT)
        own_part[order, where, 0 : 2 * lanes] = acts
        own_part[order, where, 2 * lanes : 3 * lanes] = down
        sent_part[order, where, 0 : 2 * lanes] = acts.astype(jnp.bfloat16)
        sent_part[order, where, 2 * lanes : 3 * lanes] = down.astype(jnp.bfloat16)
        part_copy(order, rel, mask).start()

    def backward_deltas(order, rel, mask):
        where = block_rows(rel, mask)
        part_copy(order, rel, mask, False).wait_recv()
        total = own_part[order, where, :] + got_part[order, where, :].astype(jnp.float32)
        gate_act, up_act = total[:, :lanes], total[:, lanes : 2 * lanes]
        delta_hidden = unscale * total[:, 2 * lanes :]
        sig = jax.nn.sigmoid(gate_act)
        made = (
            delta_hidden * up_act * sig * (1.0 + gate_act * (1.0 - sig)),
            delta_hidden * gate_act * sig,
            gate_act * sig * up_act,
        )
        for kind in range(3):
            deltas[kind * lanes : (kind + 1) * lanes, where] = made[kind].T.astype(jnp.bfloat16)

    def weight_grads(order):
        hidden = group_span(order)

        @pl.loop(0, half // tile)
        def _(index):
            columns = pl.ds(pl.multiple_of(index * tile, tile), tile)
            pair = dot(deltas[: 2 * lanes, :], tok_x[:, columns], NN).astype(jnp.bfloat16)
            grads[0, hidden, columns] = pair[:lanes]
            grads[1, hidden, columns] = pair[lanes:]
            down = unscale * dot(deltas[2 * lanes :, :], tok_c[:, columns], NN)
            grads[2, hidden, columns] = down.astype(jnp.bfloat16)

    def await_sibling(rel, mask):
        for array in range(2):
            for chunk in range(CHUNKS):
                token_arrival(array, chunk, rel, mask + 1).wait_recv()

    ready = {(0, 0): 0}
    steps = 3 * last
    for start, rel, mask in relays:
        ready[(rel, mask)] = start + 2 * CHUNKS - 1
        steps = max(steps, ready[(rel, mask)])
    own_ready = 3 * (group_rows - 1)
    done_forward, done_deltas = [], []
    for step in range(1, steps + 1):
        if step <= 3 * last:
            hop, kind = divmod(step - 1, 3)
            for direction in range(2):

                @pl.when(weight_arrives(direction, hop))
                def _(direction=direction, hop=hop, kind=kind):
                    weight_arrival(direction, hop, kind).wait_recv()

                if hop + 1 < last:

                    @pl.when(
                        jnp.logical_and(
                            weight_arrives(direction, hop), weight_sends(direction, hop + 1)
                        )
                    )
                    def _(direction=direction, hop=hop, kind=kind):
                        weight_copy(direction, hop + 1, kind).start()

        for start, rel, mask in relays:
            if start <= step < start + 2 * CHUNKS:
                array, chunk = divmod(step - start, CHUNKS)
                token_arrival(array, chunk, rel, mask).wait_recv()
                for bit in reversed(range(low_bit(mask, near_bits))):
                    token_copy(array, chunk, (rel, mask, bit)).start()
        for key in done_forward:
            if key not in done_deltas and (1 - key[0], key[1]) in done_forward:
                backward_deltas(0, *key)
                done_deltas.append(key)
        if step >= own_ready + 1:
            for key in blocks:
                if key not in done_forward and ready[key] <= step:
                    await_sibling(*key)
                    forward(0, *key)
                    done_forward.append(key)
    for key in blocks:
        if key not in done_forward:
            await_sibling(*key)
            forward(0, *key)
            done_forward.append(key)
    for key in blocks:
        if key not in done_deltas:
            backward_deltas(0, *key)
    weight_grads(0)

    grad_cuts = max(1, units // 32)
    grad_rows = units // grad_cuts

    def grad_place(unit, index):
        kind, part = index // grad_cuts, index % grad_cuts
        start = unit * units + part * grad_rows
        return kind, pl.ds(pl.multiple_of(start, grad_rows), grad_rows)

    def pass_on(going_left, unit, index):
        kind, where = grad_place(unit, index)
        landing = from_right if going_left else from_left
        direction = 0 if going_left else 1
        copy = remote(
            grads.at[kind, where],
            landing.at[kind, where],
            send_g.at[direction, unit, index],
            recv_g.at[direction, unit, index],
            left if going_left else right,
        )

        @pl.when(row < last if going_left else row > 0)
        def _():
            copy.wait_recv()
            summed = grads[kind, where, :].astype(jnp.float32) + landing[kind, where, :].astype(
                jnp.float32
            )
            grads[kind, where, :] = summed.astype(jnp.bfloat16)

        copy.start()

    def pass_units(unit):
        mirror = last - unit

        @pl.loop(0, 3 * grad_cuts)
        def _(index):
            @pl.when(jnp.logical_and(row > unit, row >= rows // 2))
            def _():
                pass_on(True, unit, index)

            @pl.when(row < mirror)
            def _():
                pass_on(False, mirror, index)

            @pl.when(jnp.logical_and(row > unit, row < rows // 2))
            def _():
                pass_on(True, unit, index)

    order_left = [last - 1] + list(range(last - 1))
    if group_rows > 1:
        pass_units(order_left[0])
    for order in range(1, groups):
        for key in blocks:
            forward(order, *key)
        for key in blocks:
            backward_deltas(order, *key)
        weight_grads(order)
    if group_rows == 1:
        pass_units(order_left[0])
    for unit in order_left[1:]:
        pass_units(unit)

    def out_copy(index):
        kind, part = index // grad_cuts, index % grad_cuts
        where = pl.ds(pl.multiple_of(part * grad_rows, grad_rows), grad_rows)
        return pltpu.make_async_copy(
            out_buf.at[kind, where], out_ref.at[kind, where], out_sem.at[index]
        )

    @pl.loop(0, 3 * grad_cuts)
    def _(index):
        kind, where = grad_place(row, index)
        acc[...] = grads[kind, where, :].astype(jnp.float32)
        for direction, landing, present in ((1, from_left, row > 0), (0, from_right, row < last)):

            @pl.when(present)
            def _(direction=direction, landing=landing):
                place = landing.at[kind, where]
                remote(
                    place,
                    place,
                    send_g.at[direction, row, index],
                    recv_g.at[direction, row, index],
                    across,
                ).wait_recv()
                acc[...] += landing[kind, where, :].astype(jnp.float32)

        part = index % grad_cuts
        to = pl.ds(pl.multiple_of(part * grad_rows, grad_rows), grad_rows)
        out_buf[kind, to, :] = acc[...].astype(jnp.bfloat16)
        out_copy(index).start()

    for kind in range(3):
        for direction in range(2):
            for hop in range(last):

                @pl.when(weight_sends(direction, hop))
                def _(kind=kind, direction=direction, hop=hop):
                    weight_copy(direction, hop, kind).wait_send()

    for array in range(2):
        for chunk in range(CHUNKS):
            for key in sends:
                token_copy(array, chunk, key).wait_send()
    for order in range(groups):
        for key in blocks:
            part_copy(order, *key).wait_send()

    @pl.loop(0, 3 * grad_cuts)
    def _(index):
        for unit in range(rows):
            kind, where = grad_place(unit, index)
            place = grads.at[kind, where]
            for direction, goes in ((0, row > unit), (1, row < unit)):

                @pl.when(goes)
                def _(direction=direction, unit=unit, place=place):
                    remote(
                        place,
                        place,
                        send_g.at[direction, unit, index],
                        recv_g.at[direction, unit, index],
                        across,
                    ).wait_send()

        out_copy(index).wait()


def per_device(rows, near_bits, x_pool, token_ids, cotangent, gate_up, down_weight, loss_exponent):
    near = 2**near_bits
    _, units, half = gate_up.shape
    per_dev = token_ids.shape[0]
    span = rows * units
    group_rows = max(1, min(rows, 128 // units))
    groups, lanes = rows // group_rows, group_rows * units
    token_count = 2 * near * per_dev
    grad_cuts = max(1, units // 32)
    sends, _ = token_plan(near_bits)
    bf16, f32 = jnp.bfloat16, jnp.float32
    anywhere = pl.BlockSpec(memory_space=pl.ANY)
    dma = pltpu.SemaphoreType.DMA
    blocks = near
    out = pl.pallas_call(
        functools.partial(kernel, near_bits, rows),
        out_shape=jax.ShapeDtypeStruct((3, units, half), bf16),
        in_specs=[
            pl.BlockSpec(memory_space=pltpu.VMEM),
            pl.BlockSpec(memory_space=pltpu.SMEM),
            anywhere,
            anywhere,
            anywhere,
            anywhere,
        ],
        out_specs=anywhere,
        scratch_shapes=[
            pltpu.VMEM((token_count, half), bf16),
            pltpu.VMEM((token_count, half), bf16),
            pltpu.VMEM((per_dev, half), bf16),
            pltpu.VMEM((x_pool.shape[0], half), bf16),
            pltpu.VMEM((3, span, half), bf16),
            pltpu.VMEM((3, span, half), bf16),
            pltpu.VMEM((3, span, half), bf16),
            pltpu.VMEM((3, span, half), bf16),
            pltpu.VMEM((groups, token_count, 3 * lanes), f32),
            pltpu.VMEM((groups, token_count, 3 * lanes), bf16),
            pltpu.VMEM((groups, token_count, 3 * lanes), bf16),
            pltpu.VMEM((3 * lanes, token_count), bf16),
            pltpu.VMEM((units // grad_cuts, half), f32),
            pltpu.VMEM((3, units, half), bf16),
            dma((2, rows - 1, 3)),
            dma((2, rows - 1, 3)),
            dma((2, CHUNKS, len(sends))),
            dma((2, CHUNKS, 2 * near)),
            dma((groups, blocks)),
            dma((groups, blocks)),
            dma((2, rows, 3 * grad_cuts)),
            dma((2, rows, 3 * grad_cuts)),
            dma((4,)),
            dma((2,)),
            dma((3 * grad_cuts,)),
        ],
        compiler_params=pltpu.CompilerParams(
            collective_id=0, has_side_effects=True, vmem_limit_bytes=67_000_000
        ),
    )(token_ids.reshape(per_dev, 1), loss_exponent, x_pool, cotangent, gate_up, down_weight)
    return out[:2], out[2]


def solution(mesh):
    rows, near_bits = line_of(mesh.shape["wide"])
    return jax.shard_map(
        functools.partial(per_device, rows, near_bits),
        mesh=mesh,
        in_specs=(
            P(("grp", "wide"), None),
            P(("grp", "wide")),
            P(("grp", "wide"), None),
            P(None, "wide", "grp"),
            P("wide", "grp"),
            P(),
        ),
        out_specs=(P(None, "wide", "grp"), P("wide", "grp")),
        check_vma=False,
    )
```

profile of v0, /device:TPU:8, one launch (start us, length us, event | category | flops | bytes accessed | tf_op | source)
XLA Modules:
  0.0 208.0 jit_solution(5915960910762229994)
XLA Ops:
  1.3 1.4 copy.8.ids_ref
  2.7 201.4 %shard_map.77 = bf16[3,64,3584]{2,1,0:T(8,128)(2,1)} custom-call(s32[128,1]{1,0:T(8,128)} %copy.8.ids_ref, s32[1]{0:T(128)S(6)} %copy.9.expo_ref, bf16[512,7168]{1,0:T(8,128)(2,1)} %pool_ref.1, bf16[128,7168]{1,0:T(8,128)(2,1)} %cot_ref.1, bf16[2,64,3584]{2,1,0:T(8,128)(2,1)} %gate_up_ref.1, bf16[64,3584]{1,0:T(8,128)(2,1)} %down_ref.1), custom_call_target="tpu_custom_call" | custom-call | tf_op jit(solution)/shard_map/pallas_call | solution.py:538
  204.1 1.8 slice_bitcast_fusion
  205.9 2.2 %slice.6 = bf16[2,64,3584]{2,1,0:T(8,128)(2,1)} slice(bf16[3,64,3584]{2,1,0:T(8,128)(2,1)} %shard_map.77), slice={[0:2], [0:64], [0:3584]} | slice | bytes 1835008 | tf_op jit(solution)/shard_map/slice | solution.py:581
where the time goes:
time: 211 us; the launch traced here: 208 us
  Pallas kernels  201 us (95%)
  local copies, waits for them, and re-layouts  5.37 us (3%)
    pallas_call x1, Pallas kernels, per_device(): pl.pallas_call(functools.partial(kernel, near_bits, rows), out_shape=jax....  201 us

commit v1 on v0

--- a/solution.py
+++ b/solution.py
@@ -50,7 +50,8 @@
     cot_ref,
     gate_up_ref,
     down_ref,
-    out_ref,
+    pair_out,
+    down_out,
     tok_x,
     tok_c,
     far_x,
@@ -85,7 +86,7 @@
     row = wide // near
     slot = wide % near
     last = rows - 1
-    per_dev, _ = ids_ref.shape
+    per_dev = ids_ref.shape[1]
     pool_rows = pool_ref.shape[0]
     half = tok_x.shape[1]
     units = gate_up_ref.shape[1]
@@ -242,7 +243,8 @@
         copy.start()
 
     first_row = (grp * wide_count + wide) * pool_rows
-    named = ids_ref[...] - first_row
+    named = (ids_ref[...] - first_row).astype(jnp.float32)
+    named = jnp.broadcast_to(named, (per_dev, per_dev)).T.astype(jnp.int32)[:, :1]
     pick = (named == lax.broadcasted_iota(jnp.int32, (per_dev, pool_rows), 1)).astype(jnp.bfloat16)
 
     def pick_into(target, offset):
@@ -325,7 +327,7 @@
         for kind in range(3):
             deltas[kind * lanes : (kind + 1) * lanes, where] = made[kind].T.astype(jnp.bfloat16)
 
-    def weight_grads(order):
+    def pair_grads(order):
         hidden = group_span(order)
 
         @pl.loop(0, half // tile)
@@ -334,6 +336,13 @@
             pair = dot(deltas[: 2 * lanes, :], tok_x[:, columns], NN).astype(jnp.bfloat16)
             grads[0, hidden, columns] = pair[:lanes]
             grads[1, hidden, columns] = pair[lanes:]
+
+    def down_grads(order):
+        hidden = group_span(order)
+
+        @pl.loop(0, half // tile)
+        def _(index):
+            columns = pl.ds(pl.multiple_of(index * tile, tile), tile)
             down = unscale * dot(deltas[2 * lanes :, :], tok_c[:, columns], NN)
             grads[2, hidden, columns] = down.astype(jnp.bfloat16)
 
@@ -343,14 +352,16 @@
                 token_arrival(array, chunk, rel, mask + 1).wait_recv()
 
     ready = {(0, 0): 0}
-    steps = 3 * last
+    deferred = groups > 1
+    weight_steps = 3 * (last - 1) if deferred else 3 * last
+    steps = weight_steps
     for start, rel, mask in relays:
         ready[(rel, mask)] = start + 2 * CHUNKS - 1
         steps = max(steps, ready[(rel, mask)])
     own_ready = 3 * (group_rows - 1)
     done_forward, done_deltas = [], []
     for step in range(1, steps + 1):
-        if step <= 3 * last:
+        if step <= weight_steps:
             hop, kind = divmod(step - 1, 3)
             for direction in range(2):
 
@@ -392,13 +403,13 @@
     for key in blocks:
         if key not in done_deltas:
             backward_deltas(0, *key)
-    weight_grads(0)
+    down_grads(0)
 
     grad_cuts = max(1, units // 32)
     grad_rows = units // grad_cuts
 
     def grad_place(unit, index):
-        kind, part = index // grad_cuts, index % grad_cuts
+        kind, part = (index // grad_cuts + 2) % 3, index % grad_cuts
         start = unit * units + part * grad_rows
         return kind, pl.ds(pl.multiple_of(start, grad_rows), grad_rows)
 
@@ -424,46 +435,16 @@
 
         copy.start()
 
-    def pass_units(unit):
-        mirror = last - unit
-
-        @pl.loop(0, 3 * grad_cuts)
-        def _(index):
-            @pl.when(jnp.logical_and(row > unit, row >= rows // 2))
-            def _():
-                pass_on(True, unit, index)
-
-            @pl.when(row < mirror)
-            def _():
-                pass_on(False, mirror, index)
-
-            @pl.when(jnp.logical_and(row > unit, row < rows // 2))
-            def _():
-                pass_on(True, unit, index)
-
-    order_left = [last - 1] + list(range(last - 1))
-    if group_rows > 1:
-        pass_units(order_left[0])
-    for order in range(1, groups):
-        for key in blocks:
-            forward(order, *key)
-        for key in blocks:
-            backward_deltas(order, *key)
-        weight_grads(order)
-    if group_rows == 1:
-        pass_units(order_left[0])
-    for unit in order_left[1:]:
-        pass_units(unit)
-
     def out_copy(index):
-        kind, part = index // grad_cuts, index % grad_cuts
-        where = pl.ds(pl.multiple_of(part * grad_rows, grad_rows), grad_rows)
-        return pltpu.make_async_copy(
-            out_buf.at[kind, where], out_ref.at[kind, where], out_sem.at[index]
-        )
-
-    @pl.loop(0, 3 * grad_cuts)
-    def _(index):
+        kind, part = (index // grad_cuts + 2) % 3, index % grad_cuts
+        to = pl.ds(pl.multiple_of(part * grad_rows, grad_rows), grad_rows)
+        pair = pltpu.make_async_copy(
+            out_buf.at[kind, to], pair_out.at[kind % 2, to], out_sem.at[index]
+        )
+        down = pltpu.make_async_copy(out_buf.at[kind, to], down_out.at[to], out_sem.at[index])
+        return kind, to, pair, down
+
+    def finish(index):
         kind, where = grad_place(row, index)
         acc[...] = grads[kind, where, :].astype(jnp.float32)
         for direction, landing, present in ((1, from_left, row > 0), (0, from_right, row < last)):
@@ -480,10 +461,75 @@
                 ).wait_recv()
                 acc[...] += landing[kind, where, :].astype(jnp.float32)
 
-        part = index % grad_cuts
-        to = pl.ds(pl.multiple_of(part * grad_rows, grad_rows), grad_rows)
+        _, to, pair, down = out_copy(index)
         out_buf[kind, to, :] = acc[...].astype(jnp.bfloat16)
-        out_copy(index).start()
+
+        @pl.when(kind < 2)
+        def _():
+            pair.start()
+
+        @pl.when(kind == 2)
+        def _():
+            down.start()
+
+    upper = row >= rows // 2
+    lower = row < rows // 2
+
+    def pass_units(unit, first=0, end=3, finishing=False):
+        mirror = last - unit
+        first, end = first * grad_cuts, end * grad_cuts
+
+        @pl.loop(first, end + 1)
+        def _(index):
+            now, later = index < end, index > first
+
+            @pl.when(jnp.logical_and(jnp.logical_and(upper, row > unit), now))
+            def _():
+                pass_on(True, unit, index)
+
+            @pl.when(jnp.logical_and(jnp.logical_and(lower, row < mirror), now))
+            def _():
+                pass_on(False, mirror, index)
+
+            @pl.when(jnp.logical_and(jnp.logical_and(upper, row < mirror), later))
+            def _():
+                pass_on(False, mirror, index - 1)
+
+            @pl.when(jnp.logical_and(jnp.logical_and(lower, row > unit), later))
+            def _():
+                pass_on(True, unit, index - 1)
+
+            if finishing:
+
+                @pl.when(later)
+                def _():
+                    finish(index - 1)
+
+    order_left = [last - 1] + list(range(last - 1))
+    if group_rows > 1:
+        pass_units(order_left[0], 0, 1, last == 1)
+    pair_grads(0)
+    if group_rows > 1:
+        pass_units(order_left[0], 1, 3, last == 1)
+    if deferred:
+        for kind in range(3):
+            for direction in range(2):
+
+                @pl.when(weight_arrives(direction, last - 1))
+                def _(direction=direction, kind=kind):
+                    weight_arrival(direction, last - 1, kind).wait_recv()
+
+    for order in range(1, groups):
+        for key in blocks:
+            forward(order, *key)
+        for key in blocks:
+            backward_deltas(order, *key)
+        down_grads(order)
+        pair_grads(order)
+    if group_rows == 1:
+        pass_units(order_left[0])
+    for unit in order_left[1:]:
+        pass_units(unit, finishing=unit == order_left[-1])
 
     for kind in range(3):
         for direction in range(2):
@@ -518,7 +564,15 @@
                         across,
                     ).wait_send()
 
-        out_copy(index).wait()
+        kind, _, pair, down = out_copy(index)
+
+        @pl.when(kind < 2)
+        def _():
+            pair.wait()
+
+        @pl.when(kind == 2)
+        def _():
+            down.wait()
 
 
 def per_device(rows, near_bits, x_pool, token_ids, cotangent, gate_up, down_weight, loss_exponent):
@@ -537,7 +591,10 @@
     blocks = near
     out = pl.pallas_call(
         functools.partial(kernel, near_bits, rows),
-        out_shape=jax.ShapeDtypeStruct((3, units, half), bf16),
+        out_shape=(
+            jax.ShapeDtypeStruct((2, units, half), bf16),
+            jax.ShapeDtypeStruct((units, half), bf16),
+        ),
         in_specs=[
             pl.BlockSpec(memory_space=pltpu.VMEM),
             pl.BlockSpec(memory_space=pltpu.SMEM),
@@ -546,7 +603,7 @@
             anywhere,
             anywhere,
         ],
-        out_specs=anywhere,
+        out_specs=(anywhere, anywhere),
         scratch_shapes=[
             pltpu.VMEM((token_count, half), bf16),
             pltpu.VMEM((token_count, half), bf16),
@@ -577,8 +634,8 @@
         compiler_params=pltpu.CompilerParams(
             collective_id=0, has_side_effects=True, vmem_limit_bytes=67_000_000
         ),
-    )(token_ids.reshape(per_dev, 1), loss_exponent, x_pool, cotangent, gate_up, down_weight)
-    return out[:2], out[2]
+    )(token_ids.reshape(1, per_dev), loss_exponent, x_pool, cotangent, gate_up, down_weight)
+    return out
 
 
 def solution(mesh):

time: 211 us -> 202 us (0.957); the launches traced: 208 us -> 201 us
  Pallas kernels: 201 us -> 196 us
    pallas_call x1, Pallas kernels: 201 us -> 196 us  [per_device(): pl.pallas_call(functools.partial(kernel, near_bits, rows), out_shape=(jax...]
    unnamed x0 -> x2, local copies, waits for them, and re-layouts: none -> 3.98 us
    slice x1 -> x0, local copies, waits for them, and re-layouts: 2.16 us -> none  [per_device(): return (out[:2], out[2])]
where the time goes in v1:
time: 202 us; the launch traced here: 201 us
  Pallas kernels  196 us (97%)
  local copies, waits for them, and re-layouts  3.98 us (2%)
    pallas_call x1, Pallas kernels, per_device(): pl.pallas_call(functools.partial(kernel, near_bits, rows), out_shape=(jax...  196 us

profile of v1, /device:TPU:8, one launch (start us, length us, event | category | flops | bytes accessed | tf_op | source)
XLA Modules:
  0.0 201.2 jit_solution(17571721605483574097)
XLA Ops:
  1.3 196.0 %shard_map.77 = (bf16[2,64,3584]{2,1,0:T(8,128)(2,1)}, bf16[64,3584]{1,0:T(8,128)(2,1)}) custom-call(s32[1,128]{1,0:T(1,128)} %bitcast.1, s32[1]{0:T(128)S(6)} %copy.10.expo_ref, bf16[512,7168]{1,0:T(8,128)(2,1)} %pool_ref.1, bf16[128,7168]{1,0:T(8,128)(2,1)} %cot_ref.1, bf16[2,64,3584]{2,1,0:T(8,128)(2,1)} %gate_up_ref.1, bf16[64,3584]{1,0:T(8,128)(2,1)} %down_ref.1), custom_call_target="tpu_custom_call" | custom-call | tf_op jit(solution)/shard_map/pallas_call | solution.py:592
  197.3 2.2 %copy.11 = bf16[2,64,3584]{2,1,0:T(8,128)(2,1)} copy(bf16[2,64,3584]{2,1,0:T(8,128)(2,1)} %get-tuple-element.4) | data formatting | bytes 1835008
  199.4 1.8 copy.12

commit v2 on v1

--- a/solution.py
+++ b/solution.py
@@ -189,8 +189,10 @@
     buffers = (tok_c, tok_x)
 
     def token_rows(rel, mask, chunk):
-        base = (grp if rel == 0 else other) * near + flipped(mask)
-        return pl.ds(pl.multiple_of(base * per_dev + chunk * cut, cut), cut)
+        core = bit_of[0] if mask % 2 == 0 else 1 - bit_of[0]
+        base = (grp if rel == 0 else other) * near + flipped(mask) - core
+        start = base * per_dev + (2 * chunk + core) * cut
+        return pl.ds(pl.multiple_of(start, cut), cut)
 
     def token_copy(array, chunk, key, source=None):
         rel, mask, bit = key
@@ -226,7 +228,8 @@
     pool_far.start()
     for chunk in range(CHUNKS):
         piece = pl.ds(chunk * cut, cut)
-        token_copy(0, chunk, ("x", 0, 0), cot_ref.at[piece, half_of(other)]).start()
+        if chunk == 0:
+            token_copy(0, chunk, ("x", 0, 0), cot_ref.at[piece, half_of(other)]).start()
         for bit in reversed(range(near_bits)):
             token_copy(0, chunk, (0, 0, bit), cot_ref.at[piece, half_of(grp)]).start()
     local = [
@@ -235,10 +238,15 @@
         )
         for kind in range(3)
     ]
-    own_rows = pl.ds(pl.multiple_of((grp * near + slot) * per_dev, per_dev), per_dev)
-    local.append(
-        pltpu.make_async_copy(cot_ref.at[:, half_of(grp)], tok_c.at[own_rows], local_sem.at[3])
-    )
+    for chunk in range(CHUNKS):
+        piece = pl.ds(chunk * cut, cut)
+        local.append(
+            pltpu.make_async_copy(
+                cot_ref.at[piece, half_of(grp)],
+                tok_c.at[token_rows(0, 0, chunk)],
+                local_sem.at[3 + chunk],
+            )
+        )
     for copy in local:
         copy.start()
 
@@ -247,22 +255,25 @@
     named = jnp.broadcast_to(named, (per_dev, per_dev)).T.astype(jnp.int32)[:, :1]
     pick = (named == lax.broadcasted_iota(jnp.int32, (per_dev, pool_rows), 1)).astype(jnp.bfloat16)
 
-    def pick_into(target, offset):
+    def pick_into(target, places):
         @pl.loop(0, half // tile)
         def _(index):
             columns = pl.ds(pl.multiple_of(index * tile, tile), tile)
-            target[pl.ds(offset, per_dev), columns] = dot(pick, pool_buf[:, columns], NN).astype(
-                jnp.bfloat16
-            )
+            picked = dot(pick, pool_buf[:, columns], NN).astype(jnp.bfloat16)
+            for chunk in range(CHUNKS):
+                target[places[chunk], columns] = picked[chunk * cut : (chunk + 1) * cut]
 
     pool_far.wait()
-    pick_into(far_x, 0)
+    pick_into(far_x, [pl.ds(chunk * cut, cut) for chunk in range(CHUNKS)])
     pool_own = pltpu.make_async_copy(pool_ref.at[:, half_of(grp)], pool_buf, pool_sem.at[1])
     pool_own.start()
     for chunk in range(CHUNKS):
-        token_copy(1, chunk, ("x", 0, 0), far_x.at[pl.ds(chunk * cut, cut)]).start()
+        piece = pl.ds(chunk * cut, cut)
+        if chunk > 0:
+            token_copy(0, chunk, ("x", 0, 0), cot_ref.at[piece, half_of(other)]).start()
+        token_copy(1, chunk, ("x", 0, 0), far_x.at[piece]).start()
     pool_own.wait()
-    pick_into(tok_x, pl.multiple_of((grp * near + slot) * per_dev, per_dev))
+    pick_into(tok_x, [token_rows(0, 0, chunk) for chunk in range(CHUNKS)])
     for chunk in range(CHUNKS):
         for bit in reversed(range(near_bits)):
             token_copy(1, chunk, (0, 0, bit)).start()
@@ -285,23 +296,25 @@
 
     blocks = [(rel, mask) for rel in range(2) for mask in range(0, near, 2)]
 
-    def part_copy(order, rel, mask, outgoing=True):
-        where = block_rows(rel, mask)
+    def part_copy(order, rel, mask, part, outgoing=True):
+        where = block_rows(rel, mask, part)
         received = (1 - rel if outgoing else rel, mask)
         return remote(
             sent_part.at[order, where],
             got_part.at[order, where],
-            send_p.at[order, blocks.index((rel, mask))],
-            recv_p.at[order, blocks.index(received)],
+            send_p.at[order, blocks.index((rel, mask)), part],
+            recv_p.at[order, blocks.index(received), part],
             across,
         )
 
-    def block_rows(rel, mask):
+    def block_rows(rel, mask, part=None):
         base = (grp if rel == 0 else other) * near + flipped(mask) - bit_of[0]
-        return pl.ds(pl.multiple_of(base * per_dev, block), block)
-
-    def forward(order, rel, mask):
-        where = block_rows(rel, mask)
+        if part is None:
+            return pl.ds(pl.multiple_of(base * per_dev, block), block)
+        return pl.ds(pl.multiple_of(base * per_dev + part * 2 * cut, 2 * cut), 2 * cut)
+
+    def forward(order, rel, mask, part=None):
+        where = block_rows(rel, mask, part)
         hidden = group_span(order)
         pair = weights[0:2, hidden, :].reshape(2 * lanes, half)
         acts = dot(tok_x[where, :], pair, NT)
@@ -310,11 +323,12 @@
         own_part[order, where, 2 * lanes : 3 * lanes] = down
         sent_part[order, where, 0 : 2 * lanes] = acts.astype(jnp.bfloat16)
         sent_part[order, where, 2 * lanes : 3 * lanes] = down.astype(jnp.bfloat16)
-        part_copy(order, rel, mask).start()
-
-    def backward_deltas(order, rel, mask):
-        where = block_rows(rel, mask)
-        part_copy(order, rel, mask, False).wait_recv()
+        for piece in range(CHUNKS) if part is None else [part]:
+            part_copy(order, rel, mask, piece).start()
+
+    def backward_deltas(order, rel, mask, part):
+        where = block_rows(rel, mask, part)
+        part_copy(order, rel, mask, part, False).wait_recv()
         total = own_part[order, where, :] + got_part[order, where, :].astype(jnp.float32)
         gate_act, up_act = total[:, :lanes], total[:, lanes : 2 * lanes]
         delta_hidden = unscale * total[:, 2 * lanes :]
@@ -346,20 +360,48 @@
             down = unscale * dot(deltas[2 * lanes :, :], tok_c[:, columns], NN)
             grads[2, hidden, columns] = down.astype(jnp.bfloat16)
 
-    def await_sibling(rel, mask):
+    def await_sibling(rel, mask, chunk):
         for array in range(2):
-            for chunk in range(CHUNKS):
-                token_arrival(array, chunk, rel, mask + 1).wait_recv()
-
-    ready = {(0, 0): 0}
+            token_arrival(array, chunk, rel, mask + 1).wait_recv()
+
+    def arrival_order(rel, index):
+        if rel == 0:
+            return divmod(index, CHUNKS)
+        chunk, array = divmod(index, 2)
+        return array, chunk
+
+    ready = {(0, 0, part): 0 for part in range(CHUNKS)}
     deferred = groups > 1
     weight_steps = 3 * (last - 1) if deferred else 3 * last
     steps = weight_steps
     for start, rel, mask in relays:
-        ready[(rel, mask)] = start + 2 * CHUNKS - 1
-        steps = max(steps, ready[(rel, mask)])
+        for index in range(2 * CHUNKS):
+            _, part = arrival_order(rel, index)
+            ready[(rel, mask, part)] = start + index
+        steps = max(steps, start + 2 * CHUNKS - 1)
+    split = relays[-1][1:]
+    pieces = [key + (part,) for key in blocks for part in range(CHUNKS)]
     own_ready = 3 * (group_rows - 1)
     done_forward, done_deltas = [], []
+
+    def advance(step):
+        for key in blocks:
+            parts = [
+                part
+                for part in range(CHUNKS)
+                if key + (part,) not in done_forward and ready[key + (part,)] <= step
+            ]
+            if not parts or (len(parts) < CHUNKS and key != split):
+                continue
+            for part in parts:
+                await_sibling(*key, part)
+                done_forward.append(key + (part,))
+            if len(parts) == CHUNKS:
+                forward(0, *key)
+            else:
+                for part in parts:
+                    forward(0, *key, part)
+
     for step in range(1, steps + 1):
         if step <= weight_steps:
             hop, kind = divmod(step - 1, 3)
@@ -381,28 +423,24 @@
 
         for start, rel, mask in relays:
             if start <= step < start + 2 * CHUNKS:
-                array, chunk = divmod(step - start, CHUNKS)
+                array, chunk = arrival_order(rel, step - start)
                 token_arrival(array, chunk, rel, mask).wait_recv()
                 for bit in reversed(range(low_bit(mask, near_bits))):
                     token_copy(array, chunk, (rel, mask, bit)).start()
-        for key in done_forward:
-            if key not in done_deltas and (1 - key[0], key[1]) in done_forward:
-                backward_deltas(0, *key)
-                done_deltas.append(key)
+        for rel, mask, part in pieces:
+            if (
+                (rel, mask, part) in done_forward
+                and (1 - rel, mask, part) in done_forward
+                and (rel, mask, part) not in done_deltas
+            ):
+                backward_deltas(0, rel, mask, part)
+                done_deltas.append((rel, mask, part))
         if step >= own_ready + 1:
-            for key in blocks:
-                if key not in done_forward and ready[key] <= step:
-                    await_sibling(*key)
-                    forward(0, *key)
-                    done_forward.append(key)
-    for key in blocks:
-        if key not in done_forward:
-            await_sibling(*key)
-            forward(0, *key)
-            done_forward.append(key)
-    for key in blocks:
-        if key not in done_deltas:
-            backward_deltas(0, *key)
+            advance(step)
+    advance(steps)
+    for rel, mask, part in pieces[::-1]:
+        if (rel, mask, part) not in done_deltas:
+            backward_deltas(0, rel, mask, part)
     down_grads(0)
 
     grad_cuts = max(1, units // 32)
@@ -475,9 +513,8 @@
     upper = row >= rows // 2
     lower = row < rows // 2
 
-    def pass_units(unit, first=0, end=3, finishing=False):
+    def pass_units(unit, first, end, finishing=False):
         mirror = last - unit
-        first, end = first * grad_cuts, end * grad_cuts
 
         @pl.loop(first, end + 1)
         def _(index):
@@ -506,11 +543,11 @@
                     finish(index - 1)
 
     order_left = [last - 1] + list(range(last - 1))
-    if group_rows > 1:
-        pass_units(order_left[0], 0, 1, last == 1)
-    pair_grads(0)
-    if group_rows > 1:
-        pass_units(order_left[0], 1, 3, last == 1)
+    total = 3 * grad_cuts
+    early = group_rows > 1
+    held_back = 1 if early and last > 1 else 0
+    if early:
+        pass_units(order_left[0], 0, grad_cuts, last == 1)
     if deferred:
         for kind in range(3):
             for direction in range(2):
@@ -519,17 +556,26 @@
                 def _(direction=direction, kind=kind):
                     weight_arrival(direction, last - 1, kind).wait_recv()
 
+    ahead = blocks[:2] if deferred else []
+    for key in ahead:
+        forward(1, *key)
+    pair_grads(0)
+    if early:
+        pass_units(order_left[0], grad_cuts, total - held_back, last == 1)
     for order in range(1, groups):
         for key in blocks:
-            forward(order, *key)
-        for key in blocks:
+            if order > 1 or key not in ahead:
+                forward(order, *key)
+        for key in pieces:
             backward_deltas(order, *key)
         down_grads(order)
         pair_grads(order)
-    if group_rows == 1:
-        pass_units(order_left[0])
+    if not early:
+        pass_units(order_left[0], 0, total)
     for unit in order_left[1:]:
-        pass_units(unit, finishing=unit == order_left[-1])
+        pass_units(unit, 0, total, unit == order_left[-1])
+    if held_back:
+        pass_units(order_left[0], total - held_back, total)
 
     for kind in range(3):
         for direction in range(2):
@@ -544,7 +590,7 @@
             for key in sends:
                 token_copy(array, chunk, key).wait_send()
     for order in range(groups):
-        for key in blocks:
+        for key in pieces:
             part_copy(order, *key).wait_send()
 
     @pl.loop(0, 3 * grad_cuts)
@@ -573,6 +619,29 @@
         @pl.when(kind == 2)
         def _():
             down.wait()
+
+
+def settle(pair_ref, down_ref, pair_out, down_out, held, come, go):
+    units = down_ref.shape[0]
+    rows = units // 2
+    moves = []
+    for index in range(6):
+        kind, where = index // 2, pl.ds(index % 2 * rows, rows)
+        source = pair_ref.at[kind, where] if kind < 2 else down_ref.at[where]
+        target = pair_out.at[kind, where] if kind < 2 else down_out.at[where]
+        moves.append(
+            (
+                pltpu.make_async_copy(source, held.at[index], come.at[index]),
+                pltpu.make_async_copy(held.at[index], target, go.at[index]),
+            )
+        )
+    for arrive, _ in moves:
+        arrive.start()
+    for arrive, leave in moves:
+        arrive.wait()
+        leave.start()
+    for _, leave in moves:
+        leave.wait()
 
 
 def per_device(rows, near_bits, x_pool, token_ids, cotangent, gate_up, down_weight, loss_exponent):
@@ -623,11 +692,11 @@
             dma((2, rows - 1, 3)),
             dma((2, CHUNKS, len(sends))),
             dma((2, CHUNKS, 2 * near)),
-            dma((groups, blocks)),
-            dma((groups, blocks)),
+            dma((groups, blocks, CHUNKS)),
+            dma((groups, blocks, CHUNKS)),
             dma((2, rows, 3 * grad_cuts)),
             dma((2, rows, 3 * grad_cuts)),
-            dma((4,)),
+            dma((3 + CHUNKS,)),
             dma((2,)),
             dma((3 * grad_cuts,)),
         ],
@@ -635,7 +704,16 @@
             collective_id=0, has_side_effects=True, vmem_limit_bytes=67_000_000
         ),
     )(token_ids.reshape(1, per_dev), loss_exponent, x_pool, cotangent, gate_up, down_weight)
-    return out
+    return pl.pallas_call(
+        settle,
+        out_shape=(
+            jax.ShapeDtypeStruct((2, units, half), bf16),
+            jax.ShapeDtypeStruct((units, half), bf16),
+        ),
+        in_specs=[anywhere, anywhere],
+        out_specs=(anywhere, anywhere),
+        scratch_shapes=[pltpu.VMEM((6, units // 2, half), bf16), dma((6,)), dma((6,))],
+    )(*out)
 
 
 def solution(mesh):

time: 202 us -> 192 us (0.950)
  Pallas kernels: 196 us -> 190 us
  local copies, waits for them, and re-layouts: 3.98 us -> 0 us
    pallas_call x1, Pallas kernels: 196 us -> 188 us  [per_device(): pl.pallas_call(functools.partial(kernel, near_bits, rows), out_shape=(jax...]
    unnamed x2 -> x0, local copies, waits for them, and re-layouts: 3.98 us -> none
    pallas_call x0 -> x1, Pallas kernels: none -> 2.22 us  [per_device(): pl.pallas_call(settle, out_shape=(jax.ShapeDtypeStruct((2, units, half),...]
where the time goes in v2:
time: 192 us
  Pallas kernels  190 us (99%)
    pallas_call x1, Pallas kernels, per_device(): pl.pallas_call(functools.partial(kernel, near_bits, rows), out_shape=(jax...  188 us

profile of v2, /device:TPU:8, one launch (start us, length us, event | category | flops | bytes accessed | tf_op | source)
XLA Modules:
  0.0 191.5 jit_solution(14836107422401098543)
XLA Ops:
  1.3 188.0 %shard_map.77 = (bf16[2,64,3584]{2,1,0:T(8,128)(2,1)}, bf16[64,3584]{1,0:T(8,128)(2,1)}) custom-call(s32[1,128]{1,0:T(1,128)} %bitcast.1, s32[1]{0:T(128)S(6)} %copy.8.expo_ref, bf16[512,7168]{1,0:T(8,128)(2,1)} %pool_ref.1, bf16[128,7168]{1,0:T(8,128)(2,1)} %cot_ref.1, bf16[2,64,3584]{2,1,0:T(8,128)(2,1)} %gate_up_ref.1, bf16[64,3584]{1,0:T(8,128)(2,1)} %down_ref.1), custom_call_target="tpu_custom_call" | custom-call | tf_op jit(solution)/shard_map/pallas_call | solution.py:661
  189.3 2.2 %shard_map.78 = (bf16[2,64,3584]{2,1,0:T(8,128)(2,1)}, bf16[64,3584]{1,0:T(8,128)(2,1)}) custom-call(bf16[2,64,3584]{2,1,0:T(8,128)(2,1)} %get-tuple-element.4.pair_ref, bf16[64,3584]{1,0:T(8,128)(2,1)} %get-tuple-element.5.down_ref), custom_call_target="tpu_custom_call" | custom-call | tf_op jit(solution)/shard_map/pallas_call | solution.py:707

commit v3 on v2

--- a/solution.py
+++ b/solution.py
@@ -96,7 +96,7 @@
     lanes = group_rows * units
     cut = per_dev // CHUNKS
     block = 2 * per_dev
-    tile = 512
+    tile = 896
 
     bit_of = [(slot // 2**bit) % 2 for bit in range(near_bits)]
 

time: 192 us -> 191 us (level)
  no operation moved by 1% of the time
where the time goes in v3:
time: 191 us
  Pallas kernels  189 us (99%)
    pallas_call x1, Pallas kernels, per_device(): pl.pallas_call(functools.partial(kernel, near_bits, rows), out_shape=(jax...  187 us

profile of v3, /device:TPU:8, one launch (start us, length us, event | category | flops | bytes accessed | tf_op | source)
XLA Modules:
  0.0 190.5 jit_solution(6480956874037773548)
XLA Ops:
  1.3 187.0 %shard_map.77 = (bf16[2,64,3584]{2,1,0:T(8,128)(2,1)}, bf16[64,3584]{1,0:T(8,128)(2,1)}) custom-call(s32[1,128]{1,0:T(1,128)} %bitcast.1, s32[1]{0:T(128)S(6)} %copy.8.expo_ref, bf16[512,7168]{1,0:T(8,128)(2,1)} %pool_ref.1, bf16[128,7168]{1,0:T(8,128)(2,1)} %cot_ref.1, bf16[2,64,3584]{2,1,0:T(8,128)(2,1)} %gate_up_ref.1, bf16[64,3584]{1,0:T(8,128)(2,1)} %down_ref.1), custom_call_target="tpu_custom_call" | custom-call | tf_op jit(solution)/shard_map/pallas_call | solution.py:661
  188.3 2.2 %shard_map.78 = (bf16[2,64,3584]{2,1,0:T(8,128)(2,1)}, bf16[64,3584]{1,0:T(8,128)(2,1)}) custom-call(bf16[2,64,3584]{2,1,0:T(8,128)(2,1)} %get-tuple-element.4.pair_ref, bf16[64,3584]{1,0:T(8,128)(2,1)} %get-tuple-element.5.down_ref), custom_call_target="tpu_custom_call" | custom-call | tf_op jit(solution)/shard_map/pallas_call | solution.py:707
